TPU v7x, 32 devices: a whole 2x2x4 slice. The times are simulated.
32 devices in a mesh: ch: 16 (over z, x, core), rep: 2 (over y).
Axes of the slice: x: 2, y: 2, z: 4, core: 2. Of those that a mesh axis runs over, the one named last changes fastest.
Arguments:
- fields_a: bfloat16 [32, 128, 4096], P('rep', 'ch'), parts along dimension 0, may hold values from -6 to 6
- latent_b: bfloat16 [32, 2048, 512], P('rep', 'ch'), parts along dimension 0, may hold values from -6 to 6
- regrid_w: bfloat16 [32, 1, 128, 64], replicated, may hold values from -0.5 to 0.5
- cell_tiles: int32 [32, 1], replicated, may hold values from 0 to 31, as said below
- norm_a: float32 [128], replicated, may hold values from 0.5 to 1.5
- enc_in: bfloat16 [128, 512], replicated, may hold values from -0.5 to 0.5
- enc_mid: bfloat16 [512, 512], replicated, may hold values from -0.25 to 0.25
- enc_out: bfloat16 [512, 512], replicated, may hold values from -0.25 to 0.25
- norm_b: float32 [512], replicated, may hold values from 0.5 to 1.5
- dec_mid: bfloat16 [512, 512], replicated, may hold values from -0.25 to 0.25
- dec_out: bfloat16 [512, 128], replicated, may hold values from -0.25 to 0.25
Outputs:
- latent_a: bfloat16 [32, 2048, 512], P('rep', 'ch'), parts along dimension 0
- cells_b: bfloat16 [32, 128, 4096], P('rep', 'ch'), parts along dimension 0
There are 2 independent parts, one for each index of `rep`. A program takes and returns all parts, laid end to end along the dimension named above; an argument that names none is the same for every part. Nothing has to cross between parts.
Inputs may be any that keep to these rules, and one draw needn't show every extreme that they name: The one column of cell_tiles names every one of the 32 cell blocks exactly once.
All inputs are finite; a program needn't handle non-finite values.
Results may differ from a plain program's by a relative error of at most 0.0066.
Values may be sent and summed in bfloat16 or wider, within the bound.
A program may use at most 64 MiB of HBM per device.

v0:
```python
import jax
import jax.numpy as jnp
from jax import lax
from jax.sharding import PartitionSpec as P

BN = 64
BC = 128
K = 1


EPSILON = 1e-05


def normalize(values, gain_vec, along):
    average = jnp.mean(values, axis=along, keepdims=True)
    centred = values - average
    spread = jnp.mean(centred * centred, axis=along, keepdims=True)
    return centred * lax.rsqrt(spread + EPSILON) * gain_vec


def shards(
    fields_a,
    latent_b,
    regrid_w,
    cell_tiles,
    norm_a,
    enc_in,
    enc_mid,
    enc_out,
    norm_b,
    dec_mid,
    dec_out,
):
    groups = lax.axis_size("ch")
    samples = fields_a.shape[0]
    own_channels = fields_a.shape[1]
    blocks_all = cell_tiles.shape[0]
    node_rows = latent_b.shape[1]
    hidden = latent_b.shape[2]
    channels = own_channels * groups
    blocks = fields_a.reshape(samples, own_channels, blocks_all, BC)
    chosen = jnp.take(blocks, cell_tiles, axis=2).reshape(samples, own_channels, blocks_all, K * BC)
    weights = regrid_w.reshape(blocks_all, K * BC, BN)
    grid_vals = jnp.einsum("ecnj,njm->ecnm", chosen, weights, preferred_element_type=jnp.float32)
    grid_sent = grid_vals.astype(jnp.bfloat16).reshape(samples, own_channels, groups, node_rows)
    received_a = lax.all_to_all(grid_sent, "ch", split_axis=2, concat_axis=1, tiled=True)
    normed = normalize(latent_b.astype(jnp.float32), norm_b, 2).astype(jnp.bfloat16)
    middle = jax.nn.silu(
        jnp.einsum("enh,hg->eng", normed, dec_mid, preferred_element_type=jnp.float32)
    ).astype(jnp.bfloat16)
    out_split = dec_out.reshape(hidden, groups, own_channels)
    decoded_sent = jnp.einsum(
        "enh,hjc->ecjn", middle, out_split, preferred_element_type=jnp.float32
    ).astype(jnp.bfloat16)
    values = received_a.reshape(samples, channels, node_rows).astype(jnp.float32)
    normed = normalize(values, norm_a[:, None], 1).astype(jnp.bfloat16)
    base = jnp.einsum("ecn,ch->enh", normed, enc_in, preferred_element_type=jnp.float32).astype(
        jnp.bfloat16
    )
    middle = jax.nn.silu(
        jnp.einsum("enh,hg->eng", base, enc_mid, preferred_element_type=jnp.float32)
    ).astype(jnp.bfloat16)
    result = base.astype(jnp.float32) + jnp.einsum(
        "enh,hg->eng", middle, enc_out, preferred_element_type=jnp.float32
    )
    latent_a = result.astype(jnp.bfloat16)
    received_b = lax.all_to_all(decoded_sent, "ch", split_axis=2, concat_axis=1, tiled=True)
    arranged = received_b.reshape(samples, groups, own_channels, node_rows)
    node_blocks = jnp.moveaxis(arranged, 1, 2).reshape(samples, own_channels, blocks_all, BN)
    inverse = jnp.argsort(cell_tiles, axis=0).T
    picked = jnp.take(node_blocks, inverse, axis=2)
    weight_sel = regrid_w[inverse, jnp.arange(K)[:, None]]
    total = jnp.einsum("ecknm,knbm->ecnb", picked, weight_sel, preferred_element_type=jnp.float32)
    cells_b = total.astype(jnp.bfloat16).reshape(samples, own_channels, blocks_all * BC)
    return (latent_a, cells_b)


def solution(mesh):
    placed = (
        P("rep", "ch", None),
        P("rep", "ch", None),
        P(),
        P(),
        P(),
        P(),
        P(),
        P(),
        P(),
        P(),
        P(),
    )
    return jax.shard_map(
        shards,
        mesh=mesh,
        in_specs=placed,
        out_specs=(P("rep", "ch", None), P("rep", "ch", None)),
        check_vma=False,
    )
```

profile of v0, /device:TPU:0, one launch (start us, length us, event | category | flops | bytes accessed | tf_op | source)
XLA Modules:
  0.0 64.0 jit_solution(9747075597492145657)
XLA Ops:
  0.6 0.0 copy-start
  0.6 0.0 copy-start.2
  0.7 0.8 %fusion.60 = s32[32]{0:T(128)S(1)} fusion(s32[32,1]{0,1:T(1,128)} %param.14), kind=kLoop, calls=%fused_computation.72 | loop fusion | flops 96 | bytes 256 | tf_op jit(solution)/shard_map/jit(_take)/broadcast_in_dim | solution.py:42
  1.4 0.7 %and_bitcast_fusion = pred[32]{0:T(512)(128)(4,1)S(1)} fusion(s32[32,1]{0,1:T(1,128)} %param.14), kind=kLoop, calls=%fused_computation.66 | loop fusion | flops 192 | bytes 160 | tf_op jit(solution)/shard_map/jit(_take)/reduce_and | solution.py:42
  2.1 0.0 copy-done
  2.1 0.9 %gather_fusion = bf16[32,16,8,128]{3,2,1,0:T(8,128)(2,1)S(1)} fusion(bf16[16,8,32,128]{3,1,2,0:T(8,128)(2,1)S(1)} %bitcast.101, s32[1024]{0:T(1024)S(1)} %pad_clamp_fusion.1), kind=kCustom, calls=%fused_computation | custom fusion | bytes 2097280 | tf_op jit(solution)/shard_map/jit(_take)/gather | solution.py:42
  3.1 0.0 copy-done.2
  3.1 0.5 fusion.14
  3.6 1.6 %copy.42 = bf16[16,8,32,64]{3,2,1,0:T(8,128)(2,1)} copy(bf16[16,8,32,64]{3,1,0,2:T(8,128)(2,1)S(1)} %fusion.14) | data formatting | bytes 1048576 | tf_op jit(solution)/shard_map/convert_element_type | solution.py:45
  5.2 0.0 copy-start.1
  5.2 2.6 %reshape.150 = bf16[16,8,16,128]{3,2,1,0:T(8,128)(2,1)} reshape(bf16[16,8,32,64]{3,2,1,0:T(8,128)(2,1)} %copy.42) | data formatting | bytes 1048576 | tf_op jit(solution)/shard_map/reshape | solution.py:45
  7.8 2.0 %copy.43 = bf16[16,8,16,128]{3,1,0,2:T(8,128)(2,1)} copy(bf16[16,8,16,128]{3,2,1,0:T(8,128)(2,1)} %reshape.150) | data formatting | bytes 1048576 | tf_op jit(solution)/shard_map/reshape | solution.py:45
  9.8 7.4 %all-to-all-start = ((bf16[16,8,16,128]{3,1,0,2:T(8,128)(2,1)}), bf16[16,8,16,128]{3,1,0,2:T(8,128)(2,1)}, u32[]{:S(2)}, u32[]{:S(2)}) async-start(bf16[16,8,16,128]{3,1,0,2:T(8,128)(2,1)} %copy.43), calls=%async_computation | async-start | bytes 1048576 | tf_op jit(solution)/shard_map/all_to_all | solution.py:46
  17.2 0.0 copy-done.1
  17.2 0.0 copy-start.5
  17.2 0.0 copy-start.8
  17.2 0.3 convert_reduce_fusion
  17.6 1.0 %fusion.2 = f32[16,128]{1,0:T(8,128)S(1)} fusion(bf16[16,128,512]{2,1,0:T(8,128)(2,1)S(1)} %copy-done.1, f32[16,128]{1,0:T(8,128)S(1)} %broadcast_multiply_fusion), kind=kLoop, calls=%fused_computation.7 | loop fusion | flops 4192256 | bytes 2113536 | tf_op jit(solution)/shard_map/reduce_sum | solution.py:17
  18.6 0.0 copy-done.5
  18.6 0.1 copy.47
  18.7 0.0 copy-done.8
  18.7 0.0 copy-start.7
  18.8 4.4 %fusion.25 = bf16[16,8,16,128]{3,2,1,0:T(8,128)(2,1)} fusion(bf16[16,128,512]{2,1,0:T(8,128)(2,1)S(1)} %copy-done.1, f32[512]{0:T(512)S(1)} %copy-done.8, f32[16,128]{1,0:T(8,128)S(1)} %add_rsqrt_fusion, f32[16,128]{1,0:T(8,128)S(1)} %broadcast_multiply_fusion, bf16[512,512]{1,0:T(8,128)(2,1)} %param.20, bf16[512,16,8]{0,2,1:T(8,128)(2,1)S(1)} %bitcast.102), kind=kOutput, calls=%fused_computation.30 | convolution fusion | flops 1352925184 | bytes 3295232 | tf_op jit(solution)/shard_map/enh,hjc->ecjn/dot_general | solution.py:52
  23.1 0.0 copy-done.7
  23.1 0.0 copy-start.3
  23.1 0.1 copy.46
  23.2 2.0 %copy.49 = bf16[16,8,16,128]{3,1,0,2:T(8,128)(2,1)} copy(bf16[16,8,16,128]{3,2,1,0:T(8,128)(2,1)} %fusion.25) | data formatting | bytes 1048576 | tf_op jit(solution)/shard_map/convert_element_type | solution.py:54
  25.3 0.8 %sort.17 = (s32[32,1]{1,0:T(8,128)}, s32[32,1]{1,0:T(8,128)S(1)}) sort(s32[32,1]{1,0:T(8,128)S(1)} %copy.46, s32[32,1]{1,0:T(8,128)S(1)} %iota.7), dimensions={0}, to_apply=%region_2.3 | sort | flops 160 | bytes 512 | tf_op jit(solution)/shard_map/jit(argsort)/sort | solution.py:70
  26.1 0.1 reduce.2
  26.2 5.3 %all-to-all-done = bf16[16,8,16,128]{3,1,0,2:T(8,128)(2,1)} async-done(((bf16[16,8,16,128]{3,1,0,2:T(8,128)(2,1)}), bf16[16,8,16,128]{3,1,0,2:T(8,128)(2,1)}, u32[]{:S(2)}, u32[]{:S(2)}) %all-to-all-start) | async-done | bytes 524320 | tf_op jit(solution)/shard_map/all_to_all | solution.py:46
  31.5 4.2 %all-to-all-start.1 = ((bf16[16,8,16,128]{3,1,0,2:T(8,128)(2,1)}), bf16[16,8,16,128]{3,1,0,2:T(8,128)(2,1)S(1)}, u32[]{:S(2)}, u32[]{:S(2)}) async-start(bf16[16,8,16,128]{3,1,0,2:T(8,128)(2,1)} %copy.49), calls=%async_computation.1 | async-start | bytes 1048576 | tf_op jit(solution)/shard_map/all_to_all | solution.py:67
  35.7 0.0 copy-done.3
  35.7 0.6 %gather_fusion.1 = bf16[32,128,64]{1,2,0:T(8,128)(2,1)S(1)} fusion(bf16[32,1,128,64]{2,3,1,0:T(8,128)(2,1)S(1)} %copy-done.3, s32[32]{0:T(128)S(1)} %or_bitcast_fusion), kind=kCustom, calls=%fused_computation.1 | custom fusion | bytes 1048832 | tf_op jit(solution)/shard_map/gather | solution.py:72
  36.4 1.1 %fusion.16 = f32[16,128]{1,0:T(8,128)S(1)} fusion(bf16[16,8,16,128]{3,1,0,2:T(8,128)(2,1)} %all-to-all-done), kind=kLoop, calls=%fused_computation.27 | loop fusion | flops 522240 | bytes 532480 | tf_op jit(solution)/shard_map/reduce_sum | solution.py:15
  37.6 1.2 %fusion.31 = f32[16,128]{1,0:T(8,128)S(1)} fusion(f32[16,128]{1,0:T(8,128)S(1)} %broadcast_multiply_fusion.1, bf16[16,8,16,128]{3,1,0,2:T(8,128)(2,1)} %all-to-all-done), kind=kLoop, calls=%fused_computation.32 | loop fusion | flops 1046528 | bytes 540672 | tf_op jit(solution)/shard_map/reduce_sum | solution.py:17
  38.8 11.2 %all-to-all-done.1 = bf16[16,8,16,128]{3,1,0,2:T(8,128)(2,1)S(1)} async-done(((bf16[16,8,16,128]{3,1,0,2:T(8,128)(2,1)}), bf16[16,8,16,128]{3,1,0,2:T(8,128)(2,1)S(1)}, u32[]{:S(2)}, u32[]{:S(2)}) %all-to-all-start.1) | async-done | bytes 524320 | tf_op jit(solution)/shard_map/all_to_all | solution.py:67
  50.0 0.3 copy.50
  50.3 0.4 reshape.153
  50.7 1.4 %copy.51 = bf16[16,8,32,64]{3,1,2,0:T(8,128)(2,1)} copy(bf16[16,8,32,64]{3,2,1,0:T(8,128)(2,1)S(1)} %reshape.153) | data formatting | bytes 1048576 | tf_op jit(solution)/shard_map/reshape | solution.py:69
  52.1 2.2 %gather_fusion.2 = bf16[32,16,8,64]{3,2,1,0:T(8,128)(2,1)S(1)} fusion(bf16[16,8,32,64]{3,1,2,0:T(8,128)(2,1)} %copy.51, s32[1024]{0:T(1024)S(1)} %pad_clamp_fusion), kind=kCustom, calls=%fused_computation.2 | custom fusion | bytes 1048704 | tf_op jit(solution)/shard_map/jit(_take)/gather | solution.py:71
  54.3 0.2 select_bitcast_fusion
  54.5 0.4 fusion.15
  54.9 0.0 copy-start.4
  54.9 0.0 copy-start.6
  54.9 0.7 %copy.53 = bf16[16,8,32,128]{3,2,1,0:T(8,128)(2,1)S(1)} copy(bf16[16,8,32,128]{3,0,1,2:T(8,128)(2,1)S(1)} %fusion.15) | data formatting | bytes 2097152 | tf_op jit(solution)/shard_map/convert_element_type | solution.py:74
  55.6 1.3 %reshape.154 = bf16[16,8,4096]{2,1,0:T(8,128)(2,1)} reshape(bf16[16,8,32,128]{3,2,1,0:T(8,128)(2,1)S(1)} %copy.53) | data formatting | bytes 2097152 | tf_op jit(solution)/shard_map/reshape | solution.py:74
  56.9 0.0 copy-done.4
  56.9 0.0 copy-done.6
  56.9 1.8 %convolution_convert_fusion = bf16[16,128,512]{2,1,0:T(8,128)(2,1)S(1)} fusion(f32[128]{0:T(128)S(1)} %copy-done.6, f32[16,128]{1,0:T(8,128)S(1)} %add_rsqrt_fusion.1, f32[16,128]{1,0:T(8,128)S(1)} %broadcast_multiply_fusion.1, bf16[16,8,16,128]{3,1,0,2:T(8,128)(2,1)} %all-to-all-done, bf16[128,512]{1,0:T(8,128)(2,1)S(1)} %copy-done.4), kind=kOutput, calls=%fused_computation.19 | convolution fusion | flops 270794752 | bytes 2769408 | tf_op jit(solution)/shard_map/ecn,ch->enh/dot_general | solution.py:57
  58.8 5.2 %add_convert_fusion = bf16[16,128,512]{2,1,0:T(8,128)(2,1)} fusion(bf16[16,128,512]{2,1,0:T(8,128)(2,1)S(1)} %convolution_convert_fusion, bf16[512,512]{1,0:T(8,128)(2,1)} %param.18, bf16[512,512]{1,0:T(8,128)(2,1)} %param.17), kind=kOutput, calls=%fused_computation.11 | convolution fusion | flops 2155872256 | bytes 5242880 | tf_op jit(solution)/shard_map/enh,hg->eng/dot_general | solution.py:63
  (11 shorter events, 0.1 us)
Async XLA Ops:
  0.6 1.5 %copy-start = (bf16[16,8,4096]{2,1,0:T(8,128)(2,1)S(1)}, bf16[16,8,4096]{2,1,0:T(8,128)(2,1)}, u32[]{:S(2)}) copy-start(bf16[16,8,4096]{2,1,0:T(8,128)(2,1)} %param.11) | copy-start | bytes 3145732
  0.6 2.4 %copy-start.2 = (bf16[32,1,128,64]{2,3,1,0:T(8,128)(2,1)S(1)}, bf16[32,1,128,64]{2,3,1,0:T(8,128)(2,1)}, u32[]{:S(2)}) copy-start(bf16[32,1,128,64]{2,3,1,0:T(8,128)(2,1)} %param.13) | copy-start | bytes 1572868
  5.2 12.0 %copy-start.1 = (bf16[16,128,512]{2,1,0:T(8,128)(2,1)S(1)}, bf16[16,128,512]{2,1,0:T(8,128)(2,1)}, u32[]{:S(2)}) copy-start(bf16[16,128,512]{2,1,0:T(8,128)(2,1)} %param.12) | copy-start | bytes 6291460
  9.8 21.8 %all-to-all-start = ((bf16[16,8,16,128]{3,1,0,2:T(8,128)(2,1)}), bf16[16,8,16,128]{3,1,0,2:T(8,128)(2,1)}, u32[]{:S(2)}, u32[]{:S(2)}) async-start(bf16[16,8,16,128]{3,1,0,2:T(8,128)(2,1)} %copy.43), calls=%async_computation | async-start | bytes 1048576 | tf_op jit(solution)/shard_map/all_to_all | solution.py:46
  17.2 1.4 %copy-start.5 = (bf16[512,128]{1,0:T(8,128)(2,1)S(1)}, bf16[512,128]{1,0:T(8,128)(2,1)}, u32[]{:S(2)}) copy-start(bf16[512,128]{1,0:T(8,128)(2,1)} %param.21) | copy-start | bytes 393220
  17.2 1.5 %copy-start.8 = (f32[512]{0:T(512)S(1)}, f32[512]{0:T(512)}, u32[]{:S(2)}) copy-start(f32[512]{0:T(512)} %param.19) | copy-start | bytes 6148
  18.7 4.4 %copy-start.7 = (s32[32,1]{0,1:T(1,128)S(1)}, s32[32,1]{0,1:T(1,128)}, u32[]{:S(2)}) copy-start(s32[32,1]{0,1:T(1,128)} %param.14) | copy-start | bytes 388
  23.1 12.6 %copy-start.3 = (bf16[32,1,128,64]{2,3,1,0:T(8,128)(2,1)S(1)}, bf16[32,1,128,64]{2,3,1,0:T(8,128)(2,1)}, u32[]{:S(2)}) copy-start(bf16[32,1,128,64]{2,3,1,0:T(8,128)(2,1)} %param.13) | copy-start | bytes 1572868
  31.5 18.4 %all-to-all-start.1 = ((bf16[16,8,16,128]{3,1,0,2:T(8,128)(2,1)}), bf16[16,8,16,128]{3,1,0,2:T(8,128)(2,1)S(1)}, u32[]{:S(2)}, u32[]{:S(2)}) async-start(bf16[16,8,16,128]{3,1,0,2:T(8,128)(2,1)} %copy.49), calls=%async_computation.1 | async-start | bytes 1048576 | tf_op jit(solution)/shard_map/all_to_all | solution.py:67
  54.9 2.0 %copy-start.4 = (bf16[128,512]{1,0:T(8,128)(2,1)S(1)}, bf16[128,512]{1,0:T(8,128)(2,1)}, u32[]{:S(2)}) copy-start(bf16[128,512]{1,0:T(8,128)(2,1)} %param.16) | copy-start | bytes 393220
  54.9 2.0 %copy-start.6 = (f32[128]{0:T(128)S(1)}, f32[128]{0:T(128)}, u32[]{:S(2)}) copy-start(f32[128]{0:T(128)} %param.15) | copy-start | bytes 1540
where the time goes:
time: 64.7 us; the launch traced here: 64 us
  waiting for transfers between devices  16.5 us (26%)
  local copies, waits for them, and re-layouts  16.4 us (25%)
  matrix products  12.4 us (19%)
  starting transfers between devices  11.6 us (18%)
  other arithmetic  6.21 us (10%)
  between operations  0.9 us (1%)
    all_to_all x1, waiting for transfers between devices, shards(): lax.all_to_all(decoded_sent, 'ch', split_axis=2, concat_axis=1, tiled=True)  11.2 us
    all_to_all x1, starting transfers between devices, shards(): lax.all_to_all(grid_sent, 'ch', split_axis=2, concat_axis=1, tiled=True)  7.44 us
    all_to_all x1, waiting for transfers between devices, shards(): lax.all_to_all(grid_sent, 'ch', split_axis=2, concat_axis=1, tiled=True)  5.32 us
    dot_general x1, matrix products, shards(): jnp.einsum('enh,hg->eng', middle, enc_out, preferred_element_type=jnp.flo...  5.25 us
    reshape x2, local copies, waits for them, and re-layouts, shards(): grid_vals.astype(jnp.bfloat16)  4.55 us
    dot_general x1, matrix products, shards(): jnp.einsum('enh,hjc->ecjn', middle, out_split, preferred_element_type=jnp...  4.37 us
    all_to_all x1, starting transfers between devices, shards(): lax.all_to_all(decoded_sent, 'ch', split_axis=2, concat_axis=1, tiled=True)  4.17 us
    reduce_sum x2, other arithmetic, normalize(): spread = jnp.mean(centred * centred, axis=along, keepdims=True)  2.17 us
  transfers between devices with their start and end apart: 2, of which 2 were waited for; matrix products, arithmetic and copies ran while one was open for 19% of the time, Pallas kernels for 0%

commit v1 on v0

v1 whole, which is shorter than its diff:
```python
import functools

import jax
import jax.numpy as jnp
from jax import lax
from jax.experimental import pallas as pl
from jax.experimental.pallas import tpu as pltpu
from jax.sharding import PartitionSpec as P

EPSILON = 1e-05
F32, BF16 = jnp.float32, jnp.bfloat16


def partner(me, step, count):
    if count & (count - 1):
        return lax.rem(me + step, count)
    result, bit = 0, 1
    while bit < count:
        mine, flip = lax.rem(me // bit, 2), lax.rem(step // bit, 2)
        result = result + (mine + flip - 2 * mine * flip) * bit
        bit *= 2
    return result


def silu(values):
    half = 0.5 * values
    return half + half * jnp.tanh(half)


def dot(left, right):
    return jnp.dot(left, right, preferred_element_type=F32)


def kernel(
    groups, samples, pieces,
    tiles, inverse,
    fields_h, latent_h, regrid_h, norm_a_h, enc_in_h, enc_mid_h, enc_out_h, norm_b_h, dec_mid_h, dec_out_h,
    latent_o, cells_o,
    fields, latent, regrid, norm_a, enc_in, enc_mid, enc_out, norm_b, dec_mid, dec_out,
    diag, send_a, recv_a, send_b, recv_b, mixed, latent_v, cells_v,
    in_sems, out_sems, send_sems, recv_sems,
):
    me = lax.axis_index("ch")
    rows, nodes = recv_a.shape[1], recv_a.shape[2]
    own = rows // samples
    bn, bc = regrid.shape[1], regrid.shape[2]
    per = nodes // bn
    blocks = regrid.shape[0]
    each = samples // pieces
    part = each * own

    loads = [
        pltpu.make_async_copy(src, dst, in_sems.at[i + 1])
        for i, (src, dst) in enumerate(
            [
                (regrid_h, regrid), (latent_h, latent), (norm_b_h, norm_b),
                (dec_mid_h, dec_mid), (dec_out_h, dec_out), (norm_a_h, norm_a), (enc_in_h, enc_in),
                (enc_mid_h, enc_mid), (enc_out_h, enc_out),
            ]
        )
    ]
    loads[0].start()

    @pl.loop(0, blocks)
    def _(block):
        pltpu.make_async_copy(
            fields_h.at[:, pl.ds(pl.multiple_of(block * bc, bc), bc)], fields.at[block], in_sems.at[0]
        ).start()

    for load in loads[1:]:
        load.start()

    barrier = pltpu.get_barrier_semaphore()

    @pl.loop(1, groups)
    def _(step):
        pl.semaphore_signal(
            barrier, inc=1, device_id={"ch": partner(me, step, groups)},
            device_id_type=pl.DeviceIdType.MESH,
        )

    def wait_all(ref, sem):
        pltpu.make_async_copy(ref, ref, sem).wait()

    wait_all(fields, in_sems.at[0])
    loads[0].wait()

    def regrid_to(owner):
        lines = []
        for k in range(per):
            sides = [jnp.zeros((bn, bc), BF16)] * per
            sides[k] = regrid[owner * per + k]
            lines.append(jnp.concatenate(sides, axis=1))
        weights = jnp.concatenate(lines, axis=0)
        diag[owner] = weights
        chosen = jnp.concatenate(
            [fields[tiles[owner * per + k]] for k in range(per)], axis=1
        )
        return lax.dot_general(
            chosen, weights, (((1,), (1,)), ((), ())), preferred_element_type=F32
        ).astype(BF16)

    recv_a[me] = regrid_to(me)

    @pl.loop(1, groups)
    def _(step):
        owner = partner(me, step, groups)
        send_a[owner] = regrid_to(owner)

    pl.semaphore_wait(barrier, groups - 1)

    @pl.loop(1, groups)
    def _(step):
        owner = partner(me, groups - step, groups)
        pltpu.make_async_remote_copy(
            src_ref=send_a.at[owner], dst_ref=recv_a.at[me],
            send_sem=send_sems.at[0], recv_sem=recv_sems.at[0],
            device_id={"ch": owner}, device_id_type=pl.DeviceIdType.MESH,
        ).start()

    for i in range(1, 5):
        loads[i].wait()
    length = each * nodes

    def decode(piece):
        values = latent[pl.ds(pl.multiple_of(piece * length, length), length), :].astype(F32)
        centred = values - jnp.mean(values, axis=1, keepdims=True)
        spread = jnp.mean(centred * centred, axis=1, keepdims=True)
        normed = (centred * lax.rsqrt(spread + EPSILON) * norm_b[...]).astype(BF16)
        middle = silu(dot(normed, dec_mid[...])).astype(BF16)
        decoded = dot(middle, dec_out[...])
        turned = [
            decoded[e * nodes : (e + 1) * nodes].T.reshape(groups, own, nodes) for e in range(each)
        ]
        send_b[piece] = jnp.concatenate(turned, axis=1).astype(BF16)
        recv_b[piece, me] = send_b[piece, me]

    def send_piece(piece):
        @pl.loop(1, groups)
        def _(step):
            owner = partner(me, groups - step, groups)
            pltpu.make_async_remote_copy(
                src_ref=send_b.at[piece, owner], dst_ref=recv_b.at[piece, me],
                send_sem=send_sems.at[1 + piece], recv_sem=recv_sems.at[1 + piece],
                device_id={"ch": owner}, device_id_type=pl.DeviceIdType.MESH,
            ).start()

    decode(0)

    @pl.loop(1, pieces)
    def _(piece):
        decode(piece)
        send_piece(piece - 1)

    for i in range(5, 9):
        loads[i].wait()
    send_piece(pieces - 1)
    wait_all(recv_a.at[pl.ds(0, groups - 1)], recv_sems.at[0])

    def written(piece):
        span = pl.ds(pl.multiple_of(piece * length, length), length)
        return pltpu.make_async_copy(latent_v.at[span], latent_o.at[span], out_sems.at[piece])

    @pl.loop(0, pieces)
    def _(piece):
        values = recv_a[:, pl.ds(pl.multiple_of(piece * part, part), part), :].astype(F32)
        lines = []
        for e in range(each):
            one = values[:, e * own : (e + 1) * own].reshape(groups * own, nodes)
            centred = one - jnp.mean(one, axis=0, keepdims=True)
            spread = jnp.mean(centred * centred, axis=0, keepdims=True)
            scaled = centred * lax.rsqrt(spread + EPSILON)
            lines.append((scaled.T * norm_a[...]).astype(BF16))
        base = dot(jnp.concatenate(lines, axis=0), enc_in[...]).astype(BF16)
        middle = silu(dot(base, enc_mid[...])).astype(BF16)
        result = base.astype(F32) + dot(middle, enc_out[...])
        latent_v[pl.ds(pl.multiple_of(piece * length, length), length), :] = result.astype(BF16)
        written(piece).start()

    for piece in range(pieces):
        wait_all(recv_b.at[piece, pl.ds(0, groups - 1)], recv_sems.at[1 + piece])

        @pl.loop(0, groups, unroll=groups <= 16)
        def _(owner):
            total = dot(recv_b[piece, owner], diag[owner]).astype(BF16)
            for k in range(per):
                mixed[owner * per + k] = total[:, k * bc : (k + 1) * bc]

        span = pl.ds(piece * part, part)

        @pl.loop(0, blocks, unroll=blocks <= 32)
        def _(block):
            cells_v[span, pl.ds(pl.multiple_of(block * bc, bc), bc)] = mixed[inverse[block]]

        pltpu.make_async_copy(cells_v.at[span], cells_o.at[span], out_sems.at[pieces + piece]).start()

    for piece in range(pieces):
        span = pl.ds(piece * part, part)
        pltpu.make_async_copy(cells_v.at[span], cells_o.at[span], out_sems.at[pieces + piece]).wait()
        written(piece).wait()
        wait_all(send_b.at[piece, pl.ds(0, groups - 1)], send_sems.at[1 + piece])
    wait_all(send_a.at[pl.ds(0, groups - 1)], send_sems.at[0])


def shards(
    fields_a, latent_b, regrid_w, cell_tiles, norm_a, enc_in, enc_mid, enc_out, norm_b, dec_mid, dec_out
):
    groups = lax.axis_size("ch")
    samples, own, cells = fields_a.shape
    nodes, hidden = latent_b.shape[1:]
    blocks, reads, bc, bn = regrid_w.shape
    assert reads == 1 and blocks % groups == 0 and nodes * groups == blocks * bn
    per = blocks // groups
    rows = samples * own
    pieces = max(p for p in (1, 2, 4) if samples % p == 0 and (rows // p) % 16 == 0)

    tiles = cell_tiles.reshape(blocks)
    order = jnp.arange(blocks, dtype=jnp.int32)
    inverse = jnp.sum(jnp.where(tiles[None, :] == order[:, None], order[None, :], 0), axis=1)
    operands = (
        fields_a.reshape(rows, cells),
        latent_b.reshape(samples * nodes, hidden),
        jnp.swapaxes(regrid_w.reshape(blocks, bc, bn), 1, 2),
        norm_a.reshape(1, -1), enc_in, enc_mid, enc_out,
        norm_b.reshape(1, -1), dec_mid, dec_out,
    )
    smem, anywhere = pl.BlockSpec(memory_space=pltpu.SMEM), pl.BlockSpec(memory_space=pl.ANY)
    latent_a, cells_b = pl.pallas_call(
        functools.partial(kernel, groups, samples, pieces),
        out_shape=(
            jax.ShapeDtypeStruct((samples * nodes, hidden), BF16),
            jax.ShapeDtypeStruct((rows, cells), BF16),
        ),
        in_specs=[smem, smem] + [anywhere] * len(operands),
        out_specs=(anywhere, anywhere),
        scratch_shapes=[pltpu.VMEM((blocks, rows, bc), BF16)]
        + [pltpu.VMEM(x.shape, x.dtype) for x in operands[1:]]
        + [
            pltpu.VMEM((groups, nodes, per * bc), BF16),
            pltpu.VMEM((groups, rows, nodes), BF16),
            pltpu.VMEM((groups, rows, nodes), BF16),
            pltpu.VMEM((pieces, groups, rows // pieces, nodes), BF16),
            pltpu.VMEM((pieces, groups, rows // pieces, nodes), BF16),
            pltpu.VMEM((blocks, rows // pieces, bc), BF16),
            pltpu.VMEM((samples * nodes, hidden), BF16),
            pltpu.VMEM((rows, cells), BF16),
            pltpu.SemaphoreType.DMA((len(operands),)),
            pltpu.SemaphoreType.DMA((2 * pieces,)),
            pltpu.SemaphoreType.DMA((1 + pieces,)),
            pltpu.SemaphoreType.DMA((1 + pieces,)),
        ],
        compiler_params=pltpu.CompilerParams(
            collective_id=0, has_side_effects=True, vmem_limit_bytes=60 * 2**20
        ),
    )(tiles, inverse, *operands)
    return latent_a.reshape(samples, nodes, hidden), cells_b.reshape(samples, own, cells)


def solution(mesh):
    split = P("rep", "ch", None)
    return jax.shard_map(
        shards,
        mesh=mesh,
        in_specs=(split, split) + (P(),) * 9,
        out_specs=(split, split),
        check_vma=False,
    )
```

time: 64.7 us -> 40.4 us (0.62)
  Pallas kernels: 0 us -> 34.1 us
  waiting for transfers between devices: 16.5 us -> 0 us
  matrix products: 12.4 us -> 0 us
  local copies, waits for them, and re-layouts: 16.4 us -> 4.16 us
  starting transfers between devices: 11.6 us -> 0 us
  other arithmetic: 6.21 us -> 1.28 us
    pallas_call x0 -> x1, Pallas kernels: none -> 34.1 us  [shards(): pl.pallas_call(functools.partial(kernel, groups, samples, pieces), out_sh...]
    all_to_all x2 -> x0, waiting for transfers between devices: 16.5 us -> none  [the longest x1 11.2 us: shards(): lax.all_to_all(decoded_sent, 'ch', split_axis=2, concat_axis=1, tiled=True)]
    dot_general x5 -> x0, matrix products: 12.4 us -> none  [the longest x1 5.25 us: shards(): jnp.einsum('enh,hg->eng', middle, enc_out, preferred_element_type=jnp.flo...]
    all_to_all x2 -> x0, starting transfers between devices: 11.6 us -> none  [the longest x1 7.44 us: shards(): lax.all_to_all(grid_sent, 'ch', split_axis=2, concat_axis=1, tiled=True)]
    reshape x5 -> x0, local copies, waits for them, and re-layouts: 7.64 us -> none  [the longest x2 4.55 us: shards(): grid_vals.astype(jnp.bfloat16)]
    convert_element_type x3 -> x0, local copies, waits for them, and re-layouts: 4.37 us -> none  [the longest x1 2.04 us: shards(): decoded_sent = jnp.einsum('enh,hjc->ecjn', middle, out_split, preferred_e...]
    unnamed x20 -> x4, local copies, waits for them, and re-layouts: 0.26 us -> 4.16 us
    gather x3 -> x0, local copies, waits for them, and re-layouts: 3.76 us -> none  [the longest x1 2.16 us: shards(): picked = jnp.take(node_blocks, inverse, axis=2)]
  transfers between devices with their start and end apart: 2 -> 0, of which waited for: 2 -> 0; matrix products, arithmetic and copies ran while one was open for 19% -> 0% of each run, Pallas kernels for 0% -> 0%
where the time goes in v1:
time: 40.4 us; the launch traced here: 40.2 us
  Pallas kernels  34.1 us (84%)
  local copies, waits for them, and re-layouts  4.16 us (10%)
  other arithmetic  1.28 us (3%)
  between operations  0.65 us (2%)
    pallas_call x1, Pallas kernels, shards(): pl.pallas_call(functools.partial(kernel, groups, samples, pieces), out_sh...  34.1 us
    unnamed x4, local copies, waits for them, and re-layouts  4.16 us
    reduce_sum x1, other arithmetic, shards(): jnp.sum(jnp.where(tiles[None, :] == order[:, None], order[None, :], 0), a...  1.28 us

profile of v1, /device:TPU:0, one launch (start us, length us, event | category | flops | bytes accessed | tf_op | source)
XLA Modules:
  0.0 40.2 jit_solution(2000169814982382732)
XLA Ops:
  0.6 1.3 %select_reduce_fusion.inverse = s32[32]{0:T(128)} fusion(s32[32]{0:T(128)} %bitcast.16), kind=kLoop, calls=%fused_computation | loop fusion | flops 3040 | bytes 256 | tf_op jit(solution)/shard_map/reduce_sum | solution.py:219
  1.9 34.1 %shard_map.122 = (bf16[2048,512]{1,0:T(8,128)(2,1)}, bf16[128,4096]{1,0:T(8,128)(2,1)}) custom-call(s32[32]{0:T(128)} %bitcast.17, s32[32]{0:T(128)} %select_reduce_fusion.inverse, bf16[128,4096]{1,0:T(8,128)(2,1)} %bitcast.13, bf16[2048,512]{1,0:T(8,128)(2,1)} %bitcast.10, bf16[32,64,128]{2,1,0:T(8,128)(2,1)} %bitcast.14, f32[1,128]{1,0:T(1,128)} %bitcast.18, ...), custom_call_target="tpu_custom_call" | custom-call | tf_op jit(solution)/shard_map/pallas_call | solution.py:228
  36.0 0.0 copy-start
  36.0 3.2 %copy.15 = bf16[16,128,512]{2,1,0:T(8,128)(2,1)} copy(bf16[16,128,512]{2,1,0:T(8,128)(2,1)} %bitcast.11) | data formatting | bytes 4194304
  39.2 0.0 copy-done
  39.2 1.0 %copy.16 = bf16[16,8,4096]{2,1,0:T(8,128)(2,1)} copy(bf16[16,8,4096]{2,1,0:T(8,128)(2,1)S(1)} %bitcast.12) | data formatting | bytes 2097152
Async XLA Ops:
  36.0 3.2 %copy-start = (bf16[128,4096]{1,0:T(8,128)(2,1)S(1)}, bf16[128,4096]{1,0:T(8,128)(2,1)}, u32[]{:S(2)}) copy-start(bf16[128,4096]{1,0:T(8,128)(2,1)} %get-tuple-element.5) | copy-start | bytes 3145732

commit v2 on v1

--- a/solution.py
+++ b/solution.py
@@ -8,6 +8,7 @@
 from jax.sharding import PartitionSpec as P
 
 EPSILON = 1e-05
+VMEM_BYTES = 67043328
 F32, BF16 = jnp.float32, jnp.bfloat16
 
 
@@ -33,12 +34,12 @@
 
 def kernel(
     groups, samples, pieces,
-    tiles, inverse,
+    tiles, tiles_h,
     fields_h, latent_h, regrid_h, norm_a_h, enc_in_h, enc_mid_h, enc_out_h, norm_b_h, dec_mid_h, dec_out_h,
-    latent_o, cells_o,
+    latent_v, mixed, tiles_v,
     fields, latent, regrid, norm_a, enc_in, enc_mid, enc_out, norm_b, dec_mid, dec_out,
-    diag, send_a, recv_a, send_b, recv_b, mixed, latent_v, cells_v,
-    in_sems, out_sems, send_sems, recv_sems,
+    diag, send_a, recv_a, send_b, recv_b,
+    in_sems, send_sems, recv_sems,
 ):
     me = lax.axis_index("ch")
     rows, nodes = recv_a.shape[1], recv_a.shape[2]
@@ -55,7 +56,7 @@
             [
                 (regrid_h, regrid), (latent_h, latent), (norm_b_h, norm_b),
                 (dec_mid_h, dec_mid), (dec_out_h, dec_out), (norm_a_h, norm_a), (enc_in_h, enc_in),
-                (enc_mid_h, enc_mid), (enc_out_h, enc_out),
+                (enc_mid_h, enc_mid), (enc_out_h, enc_out), (tiles_h, tiles_v),
             ]
         )
     ]
@@ -152,14 +153,10 @@
         decode(piece)
         send_piece(piece - 1)
 
-    for i in range(5, 9):
+    for i in range(5, 10):
         loads[i].wait()
     send_piece(pieces - 1)
     wait_all(recv_a.at[pl.ds(0, groups - 1)], recv_sems.at[0])
-
-    def written(piece):
-        span = pl.ds(pl.multiple_of(piece * length, length), length)
-        return pltpu.make_async_copy(latent_v.at[span], latent_o.at[span], out_sems.at[piece])
 
     @pl.loop(0, pieces)
     def _(piece):
@@ -175,7 +172,6 @@
         middle = silu(dot(base, enc_mid[...])).astype(BF16)
         result = base.astype(F32) + dot(middle, enc_out[...])
         latent_v[pl.ds(pl.multiple_of(piece * length, length), length), :] = result.astype(BF16)
-        written(piece).start()
 
     for piece in range(pieces):
         wait_all(recv_b.at[piece, pl.ds(0, groups - 1)], recv_sems.at[1 + piece])
@@ -184,22 +180,29 @@
         def _(owner):
             total = dot(recv_b[piece, owner], diag[owner]).astype(BF16)
             for k in range(per):
-                mixed[owner * per + k] = total[:, k * bc : (k + 1) * bc]
-
-        span = pl.ds(piece * part, part)
-
-        @pl.loop(0, blocks, unroll=blocks <= 32)
-        def _(block):
-            cells_v[span, pl.ds(pl.multiple_of(block * bc, bc), bc)] = mixed[inverse[block]]
-
-        pltpu.make_async_copy(cells_v.at[span], cells_o.at[span], out_sems.at[pieces + piece]).start()
+                mixed[owner * per + k, pl.ds(piece * part, part), :] = total[:, k * bc : (k + 1) * bc]
 
     for piece in range(pieces):
-        span = pl.ds(piece * part, part)
-        pltpu.make_async_copy(cells_v.at[span], cells_o.at[span], out_sems.at[pieces + piece]).wait()
-        written(piece).wait()
         wait_all(send_b.at[piece, pl.ds(0, groups - 1)], send_sems.at[1 + piece])
     wait_all(send_a.at[pl.ds(0, groups - 1)], send_sems.at[0])
+
+
+def place(tiles_h, latent_v, mixed, latent_o, cells_o, tiles, sems):
+    blocks, _, bc = mixed.shape
+    fetch = pltpu.make_async_copy(tiles_h, tiles, sems.at[2])
+    fetch.start()
+    copy = pltpu.make_async_copy(latent_v, latent_o, sems.at[0])
+    copy.start()
+    fetch.wait()
+
+    @pl.loop(0, blocks, unroll=blocks <= 32)
+    def _(block):
+        pltpu.make_async_copy(
+            mixed.at[block], cells_o.at[:, pl.ds(pl.multiple_of(tiles[0, block] * bc, bc), bc)], sems.at[1]
+        ).start()
+
+    pltpu.make_async_copy(mixed, mixed, sems.at[1]).wait()
+    copy.wait()
 
 
 def shards(
@@ -215,8 +218,6 @@
     pieces = max(p for p in (1, 2, 4) if samples % p == 0 and (rows // p) % 16 == 0)
 
     tiles = cell_tiles.reshape(blocks)
-    order = jnp.arange(blocks, dtype=jnp.int32)
-    inverse = jnp.sum(jnp.where(tiles[None, :] == order[:, None], order[None, :], 0), axis=1)
     operands = (
         fields_a.reshape(rows, cells),
         latent_b.reshape(samples * nodes, hidden),
@@ -224,15 +225,17 @@
         norm_a.reshape(1, -1), enc_in, enc_mid, enc_out,
         norm_b.reshape(1, -1), dec_mid, dec_out,
     )
-    smem, anywhere = pl.BlockSpec(memory_space=pltpu.SMEM), pl.BlockSpec(memory_space=pl.ANY)
-    latent_a, cells_b = pl.pallas_call(
+    smem, vmem = pl.BlockSpec(memory_space=pltpu.SMEM), pl.BlockSpec(memory_space=pltpu.VMEM)
+    hbm = pl.BlockSpec(memory_space=pltpu.HBM)
+    latent_v, mixed, tiles_v = pl.pallas_call(
         functools.partial(kernel, groups, samples, pieces),
         out_shape=(
-            jax.ShapeDtypeStruct((samples * nodes, hidden), BF16),
-            jax.ShapeDtypeStruct((rows, cells), BF16),
+            pltpu.VMEM((samples * nodes, hidden), BF16),
+            pltpu.VMEM((blocks, rows, bc), BF16),
+            pltpu.VMEM((1, blocks), jnp.int32),
         ),
-        in_specs=[smem, smem] + [anywhere] * len(operands),
-        out_specs=(anywhere, anywhere),
+        in_specs=[smem, hbm] + [hbm] * len(operands),
+        out_specs=(vmem, vmem, vmem),
         scratch_shapes=[pltpu.VMEM((blocks, rows, bc), BF16)]
         + [pltpu.VMEM(x.shape, x.dtype) for x in operands[1:]]
         + [
@@ -241,18 +244,25 @@
             pltpu.VMEM((groups, rows, nodes), BF16),
             pltpu.VMEM((pieces, groups, rows // pieces, nodes), BF16),
             pltpu.VMEM((pieces, groups, rows // pieces, nodes), BF16),
-            pltpu.VMEM((blocks, rows // pieces, bc), BF16),
-            pltpu.VMEM((samples * nodes, hidden), BF16),
-            pltpu.VMEM((rows, cells), BF16),
-            pltpu.SemaphoreType.DMA((len(operands),)),
-            pltpu.SemaphoreType.DMA((2 * pieces,)),
+            pltpu.SemaphoreType.DMA((len(operands) + 1,)),
             pltpu.SemaphoreType.DMA((1 + pieces,)),
             pltpu.SemaphoreType.DMA((1 + pieces,)),
         ],
         compiler_params=pltpu.CompilerParams(
-            collective_id=0, has_side_effects=True, vmem_limit_bytes=60 * 2**20
+            collective_id=0, has_side_effects=True, vmem_limit_bytes=VMEM_BYTES - 2 * (samples * nodes * hidden + rows * cells) - 2**14
         ),
-    )(tiles, inverse, *operands)
+    )(tiles, tiles.reshape(1, blocks), *operands)
+    latent_a, cells_b = pl.pallas_call(
+        place,
+        out_shape=(
+            jax.ShapeDtypeStruct((samples * nodes, hidden), BF16),
+            jax.ShapeDtypeStruct((rows, cells), BF16),
+        ),
+        in_specs=[vmem, vmem, vmem],
+        out_specs=(hbm, hbm),
+        scratch_shapes=[pltpu.SMEM((1, blocks), jnp.int32), pltpu.SemaphoreType.DMA((3,))],
+        compiler_params=pltpu.CompilerParams(vmem_limit_bytes=16 * 2**20),
+    )(tiles_v, latent_v, mixed)
     return latent_a.reshape(samples, nodes, hidden), cells_b.reshape(samples, own, cells)
 
 

time: 40.4 us -> 35.8 us (0.89)
  local copies, waits for them, and re-layouts: 4.16 us -> 0 us
  other arithmetic: 1.28 us -> 0 us
  Pallas kernels: 34.1 us -> 35 us
    unnamed x4 -> x0, local copies, waits for them, and re-layouts: 4.16 us -> none
    pallas_call x0 -> x1, Pallas kernels: none -> 1.66 us  [shards(): pl.pallas_call(place, out_shape=(jax.ShapeDtypeStruct((samples * nodes, h...]
    reduce_sum x1 -> x0, other arithmetic: 1.28 us -> none  [shards(): jnp.sum(jnp.where(tiles[None, :] == order[:, None], order[None, :], 0), a...]
    pallas_call x1, Pallas kernels: 34.1 us -> 33.3 us  [shards(): pl.pallas_call(functools.partial(kernel, groups, samples, pieces), out_sh...]
where the time goes in v2:
time: 35.8 us; the launch traced here: 35.6 us
  Pallas kernels  35 us (98%)
  between operations  0.64 us (2%)
    pallas_call x1, Pallas kernels, shards(): pl.pallas_call(functools.partial(kernel, groups, samples, pieces), out_sh...  33.3 us
    pallas_call x1, Pallas kernels, shards(): pl.pallas_call(place, out_shape=(jax.ShapeDtypeStruct((samples * nodes, h...  1.66 us

profile of v2, /device:TPU:0, one launch (start us, length us, event | category | flops | bytes accessed | tf_op | source)
XLA Modules:
  0.0 35.6 jit_solution(13561327026819874600)
XLA Ops:
  0.6 33.3 %shard_map.122 = (bf16[2048,512]{1,0:T(8,128)(2,1)S(1)}, bf16[32,128,128]{2,1,0:T(8,128)(2,1)S(1)}, s32[1,32]{1,0:T(1,128)S(1)}) custom-call(s32[32]{0:T(128)} %bitcast.15, s32[1,32]{1,0:T(1,128)} %bitcast.16, bf16[128,4096]{1,0:T(8,128)(2,1)} %bitcast.12, bf16[2048,512]{1,0:T(8,128)(2,1)} %bitcast.11, bf16[32,64,128]{2,1,0:T(8,128)(2,1)} %bitcast.13, ...), custom_call_target="tpu_custom_call" | custom-call | tf_op jit(solution)/shard_map/pallas_call | solution.py:230
  33.9 1.7 %shard_map.123 = (bf16[2048,512]{1,0:T(8,128)(2,1)}, bf16[128,4096]{1,0:T(8,128)(2,1)}) custom-call(s32[1,32]{1,0:T(1,128)S(1)} %get-tuple-element.7.tiles_h, bf16[2048,512]{1,0:T(8,128)(2,1)S(1)} %get-tuple-element.8.latent_v, bf16[32,128,128]{2,1,0:T(8,128)(2,1)S(1)} %get-tuple-element.9.mixed), custom_call_target="tpu_custom_call" | custom-call | tf_op jit(solution)/shard_map/pallas_call | solution.py:255
